TPU v7x, 32 devices: a whole 2x2x4 slice. The times are simulated.
32 devices in a mesh: dp: 4 (over y, x), row: 4 (over z), col: 2 (over core).
Axes of the slice: x: 2, y: 2, z: 4, core: 2. Of those that a mesh axis runs over, the one named last changes fastest.
Arguments:
- activations: bfloat16 [4, 64, 128, 512], P('dp', None, 'row', 'col'), may hold values from -18 to 18
- kernel: bfloat16 [3, 3, 64, 64], replicated, may hold values from -0.125 to 0.125
- gain: float32 [64], replicated, may hold values from 0.25 to 1.75
- cotangent: bfloat16 [4, 64, 128, 512], P('dp', None, 'row', 'col'), may hold values from -16 to 16
Outputs:
- input_grad: bfloat16 [4, 64, 128, 512], P('dp', None, 'row', 'col')
- weight_grad: float32 [3, 3, 64, 64], P(None, None, 'dp')
- gain_grad: float32 [64], replicated
- shift_grad: float32 [64], replicated
All inputs are finite; a program needn't handle non-finite values.
Results may differ from a plain program's by a relative error of at most 0.0049.
Values may be sent and summed in bfloat16 or wider, within the bound.
A program may use at most 64 MiB of HBM per device.

v0:
```python
import jax
import jax.numpy as jnp
from jax import lax
from jax.sharding import PartitionSpec as P


def with_halo(shard, sides, width):
    for axis, dim in sides:
        count, length = (lax.axis_size(axis), shard.shape[dim])
        up = [(i, (i + 1) % count) for i in range(count - 1)]
        down = [(j, i) for i, j in up]
        last = lax.slice_in_dim(shard, length - width, length, axis=dim)
        initial = lax.slice_in_dim(shard, 0, width, axis=dim)
        before = lax.ppermute(last, axis, up)
        after = lax.ppermute(initial, axis, down)
        shard = jnp.concatenate([before, shard, after], axis=dim)
    return shard


def per_device(activations, kernel, gain, cotangent):
    images, channels, height, width = activations.shape
    total = jnp.float32(
        images * height * width * lax.axis_size("dp") * lax.axis_size("row") * lax.axis_size("col")
    )
    padded = with_halo(activations, (("row", 2), ("col", 3)), 1)
    pre = jnp.zeros((images, channels, height, width), jnp.float32)
    for tap_row in range(3):
        for tap_col in range(3):
            window = padded[:, :, tap_row : tap_row + height, tap_col : tap_col + width]
            pre = pre + jnp.einsum(
                "oc,bchw->bohw",
                kernel[tap_row, tap_col],
                window,
                preferred_element_type=jnp.float32,
            )
    grad = cotangent.astype(jnp.float32)
    local_pre = jnp.sum(pre, axis=(0, 2, 3))
    local_sq = jnp.sum(pre * pre, axis=(0, 2, 3))
    local_cot = jnp.sum(grad, axis=(0, 2, 3))
    local_cross = jnp.sum(grad * pre, axis=(0, 2, 3))
    sum_pre, sum_sq, sum_cot, sum_cross = lax.psum(
        (local_pre, local_sq, local_cot, local_cross), ("dp", "row", "col")
    )
    mean = sum_pre / total
    rstd = lax.rsqrt(sum_sq / total - mean * mean + 1e-05)
    sum_norm = (sum_cross - mean * sum_cot) * rstd
    normed = (pre - mean[:, None, None]) * rstd[:, None, None]
    pre_grad = (gain * rstd)[:, None, None] * (
        grad - (sum_cot / total)[:, None, None] - normed * (sum_norm / total)[:, None, None]
    )
    pre_grad = pre_grad.astype(jnp.bfloat16)
    grad_padded = with_halo(pre_grad, (("row", 2), ("col", 3)), 1)
    input_grad = jnp.zeros((images, channels, height, width), jnp.float32)
    kernel_terms = []
    for tap_row in range(3):
        for tap_col in range(3):
            shifted = grad_padded[
                :, :, 2 - tap_row : 2 - tap_row + height, 2 - tap_col : 2 - tap_col + width
            ]
            input_grad = input_grad + jnp.einsum(
                "oc,bohw->bchw",
                kernel[tap_row, tap_col],
                shifted,
                preferred_element_type=jnp.float32,
            )
            window = padded[:, :, tap_row : tap_row + height, tap_col : tap_col + width]
            kernel_terms.append(
                jnp.einsum("bohw,bchw->oc", pre_grad, window, preferred_element_type=jnp.float32)
            )
    factor = total ** (-0.5)
    local_kernel = jnp.stack(kernel_terms).reshape(3, 3, channels, channels) * factor
    spatial = lax.psum(local_kernel, ("row", "col"))
    weight_grad = lax.psum_scatter(spatial, "dp", scatter_dimension=2, tiled=True)
    return (input_grad.astype(jnp.bfloat16), weight_grad, sum_norm / total, sum_cot / total)


def solution(mesh):
    return jax.shard_map(
        per_device,
        mesh=mesh,
        in_specs=(P("dp", None, "row", "col"), P(), P(), P("dp", None, "row", "col")),
        out_specs=(P("dp", None, "row", "col"), P(None, None, "dp", None), P(), P()),
        check_vma=False,
    )
```

profile of v0, /device:TPU:0, one launch (start us, length us, event | category | flops | bytes accessed | tf_op | source)
XLA Modules:
  0.0 162.4 jit_solution(4085869104326707929)
XLA Ops:
  7.2 1.9 %copy.26 = bf16[1,64,32,256]{3,1,2,0:T(8,128)(2,1)S(1)} copy(bf16[1,64,32,256]{3,2,1,0:T(8,128)(2,1)} %param.4) | data formatting | bytes 2097152 | tf_op args[0]
  9.2 5.0 %collective-permute-start = (bf16[1,64,1,256]{3,1,2,0:T(8,128)(2,1)S(1)}, bf16[1,64,1,256]{3,1,2,0:T(8,128)(2,1)S(1)}, u32[]{:S(2)}, u32[]{:S(2)}) collective-permute-start(bf16[1,64,1,256]{3,1,2,0:T(8,128)(2,1)S(1)} %get-tuple-element.29), channel_id=1, source_target_pairs={{0,2},{2,4},{4,6},{1,3},{3,5},{5,7},{8,10},{10,12},{12,14},{9,11},... | collective-permute-start | bytes 98312 | tf_op jit(solution)/shard_map/ppermute | solution.py:14
  14.1 1.3 collective-permute-start.1
  15.4 2.2 %fusion.55 = f32[32,256,64]{1,2,0:T(8,128)} fusion(bf16[64,32,256]{2,1,0:T(8,128)(2,1)S(1)} %bitcast.222, bf16[3,3,64,64]{3,2,1,0:T(8,128)(2,1)S(1)} %copy-done.18), kind=kOutput, calls=%fused_computation.92 | convolution fusion | flops 67108864 | bytes 3162112 | tf_op jit(solution)/shard_map/oc,bchw->bohw/dot_general | solution.py:30
  18.3 1.7 %collective-permute-done.1 = bf16[1,64,1,256]{3,1,2,0:T(8,128)(2,1)S(1)} collective-permute-done((bf16[1,64,1,256]{3,1,2,0:T(8,128)(2,1)S(1)}, bf16[1,64,1,256]{3,1,2,0:T(8,128)(2,1)S(1)}, u32[]{:S(2)}, u32[]{:S(2)}) %collective-permute-start.1) | collective-permute-done | bytes 32800 | tf_op jit(solution)/shard_map/ppermute | solution.py:15
  20.6 1.3 collective-permute-start.3
  22.2 3.0 %collective-permute-start.2 = (bf16[1,64,34,1]{1,2,3,0:T(8,128)(2,1)S(1)}, bf16[1,64,34,1]{1,2,3,0:T(8,128)(2,1)S(1)}, u32[]{:S(2)}, u32[]{:S(2)}) collective-permute-start(bf16[1,64,34,1]{1,2,3,0:T(8,128)(2,1)S(1)} %copy.29), channel_id=1, source_target_pairs={{0,1},{2,3},{4,5},{6,7},{8,9},{10,11},{12,13},{14,15},{16,17},{18,... | collective-permute-start | bytes 13064 | tf_op jit(solution)/shard_map/ppermute | solution.py:14
  25.2 1.8 %fusion.58 = f32[32,256,64]{1,2,0:T(8,128)} fusion(bf16[1,64,32,256]{3,1,2,0:T(8,128)(2,1)S(1)} %copy.26, bf16[1,64,1,256]{3,1,2,0:T(8,128)(2,1)S(1)} %collective-permute-done, bf16[3,3,64,64]{3,2,1,0:T(8,128)(2,1)S(1)} %copy-done.18), kind=kOutput, calls=%fused_computation.94 | convolution fusion | flops 69206016 | bytes 3194880 | tf_op jit(solution)/shard_map/oc,bchw->bohw/dot_general | solution.py:30
  27.0 1.7 %fusion.61 = f32[32,256,64]{1,2,0:T(8,128)} fusion(bf16[1,64,1,256]{3,1,2,0:T(8,128)(2,1)S(1)} %collective-permute-done.1, bf16[1,64,32,256]{3,1,2,0:T(8,128)(2,1)S(1)} %copy.26, bf16[3,3,64,64]{3,2,1,0:T(8,128)(2,1)S(1)} %copy-done.18), kind=kOutput, calls=%fused_computation.95 | convolution fusion | flops 69206016 | bytes 3194880 | tf_op jit(solution)/shard_map/oc,bchw->bohw/dot_general | solution.py:30
  29.1 2.1 %fusion.78 = f32[32,256,64]{1,2,0:T(8,128)} fusion(bf16[3,3,64,64]{3,2,1,0:T(8,128)(2,1)S(1)} %copy-done.18, bf16[1,64,34,256]{3,1,2,0:T(8,128)(2,1)S(1)} %constant_dynamic-update-slice_fusion, bf16[1,64,34,1]{3,1,2,0:T(8,128)(2,1)S(1)} %copy.33), kind=kOutput, calls=%fused_computation.109 | convolution fusion | flops 69206016 | bytes 3784704 | tf_op jit(solution)/shard_map/oc,bchw->bohw/dot_general | solution.py:30
  31.1 2.1 %fusion.86 = f32[32,256,64]{1,2,0:T(8,128)} fusion(bf16[3,3,64,64]{3,2,1,0:T(8,128)(2,1)S(1)} %copy-done.18, bf16[1,64,34,256]{3,1,2,0:T(8,128)(2,1)S(1)} %constant_dynamic-update-slice_fusion, bf16[1,64,34,1]{3,1,2,0:T(8,128)(2,1)S(1)} %copy.33), kind=kOutput, calls=%fused_computation.117 | convolution fusion | flops 69206016 | bytes 3784704 | tf_op jit(solution)/shard_map/oc,bchw->bohw/dot_general | solution.py:30
  36.0 0.7 copy-done.14
  37.5 0.7 copy-done.11
  38.3 3.8 %fusion.3 = (f32[64]{0:T(128)S(1)}, f32[64]{0:T(128)S(1)}, f32[64]{0:T(128)S(1)}, f32[32,256,64]{1,2,0:T(8,128)S(1)}) fusion(bf16[1,64,32,256]{3,2,1,0:T(8,128)(2,1)} %param.7, bf16[1,64,34,1]{3,1,2,0:T(8,128)(2,1)S(1)} %copy-done.2, bf16[1,64,34,256]{3,1,2,0:T(8,128)(2,1)S(1)} %constant_dynamic-update-slice_fusion, ...), kind=kOutput, calls=%fused_computation.6 | convolution fusion | flops 76545856 | bytes 21611264 | tf_op jit(solution)/shard_map/oc,bchw->bohw/dot_general | solution.py:30
  42.3 40.6 %all-reduce = (f32[64]{0:T(128)S(1)}, f32[64]{0:T(128)S(1)}, f32[64]{0:T(128)S(1)}, f32[64]{0:T(128)S(1)}) all-reduce(f32[64]{0:T(128)S(1)} %get-tuple-element.13, f32[64]{0:T(128)S(1)} %reduce_sum.37, f32[64]{0:T(128)S(1)} %get-tuple-element.12, f32[64]{0:T(128)S(1)} %get-tuple-element.14), channel_id=1, replica_groups=mesh['dp'=4,'row'=4,'col'=2] {'dp','row','col'}, use_global_device_ids=true, to_apply=%region_1.0 | all-reduce | flops 256 | bytes 2048 | tf_op jit(solution)/shard_map/psum | solution.py:41
  83.0 2.8 %fusion.2 = bf16[1,64,32,256]{3,1,2,0:T(8,128)(2,1)S(1)} fusion(f32[32,256,64]{1,2,0:T(8,128)} %copy-done, f32[64]{0:T(128)S(1)} %get-tuple-element.32, f32[64]{0:T(128)S(1)} %get-tuple-element.20, f32[64]{0:T(128)S(1)} %get-tuple-element.33, f32[64]{0:T(128)S(1)} %get-tuple-element.31, f32[64]{0:T(128)S(1)} %get-tuple-element.19, ...), kind=kLoop, calls=%fused_computation.5 | loop fusion | flops 4194304 | bytes 4195584 | tf_op jit(solution)/shard_map/convert_element_type | solution.py:51
  86.4 1.8 %fusion.52 = f32[32,256,64]{1,2,0:T(8,128)} fusion(bf16[1,64,32,256]{3,1,2,0:T(8,128)(2,1)S(1)} %fusion.2, bf16[3,3,64,64]{3,2,1,0:T(8,128)(2,1)S(1)} %copy-done.18), kind=kOutput, calls=%fused_computation.89 | convolution fusion | flops 67108864 | bytes 3162112 | tf_op jit(solution)/shard_map/oc,bohw->bchw/dot_general | solution.py:60
  91.2 1.3 fusion.11
  95.0 1.3 collective-permute-start.5
  96.3 4.5 %collective-permute-start.4 = (bf16[1,64,1,256]{3,1,2,0:T(8,128)(2,1)S(1)}, bf16[1,64,1,256]{3,1,2,0:T(8,128)(2,1)S(1)}, u32[]{:S(2)}, u32[]{:S(2)}) collective-permute-start(bf16[1,64,1,256]{3,1,2,0:T(8,128)(2,1)S(1)} %get-tuple-element.28), channel_id=1, source_target_pairs={{0,2},{2,4},{4,6},{1,3},{3,5},{5,7},{8,10},{10,12},{12,14},{9,11},... | collective-permute-start | bytes 98312 | tf_op jit(solution)/shard_map/ppermute | solution.py:14
  100.9 0.8 broadcast_multiply_fusion
  101.6 0.8 collective-permute-done.4
  103.2 1.3 collective-permute-start.6
  104.8 3.2 %collective-permute-start.7 = (bf16[1,64,34,1]{1,2,3,0:T(8,128)(2,1)S(1)}, bf16[1,64,34,1]{1,2,3,0:T(8,128)(2,1)S(1)}, u32[]{:S(2)}, u32[]{:S(2)}) collective-permute-start(bf16[1,64,34,1]{1,2,3,0:T(8,128)(2,1)S(1)} %copy.41), channel_id=1, source_target_pairs={{0,1},{2,3},{4,5},{6,7},{8,9},{10,11},{12,13},{14,15},{16,17},{18,... | collective-permute-start | bytes 13064 | tf_op jit(solution)/shard_map/ppermute | solution.py:14
  108.1 1.8 %fusion.35 = f32[32,256,64]{1,2,0:T(8,128)} fusion(bf16[1,64,1,256]{3,1,2,0:T(8,128)(2,1)S(1)} %collective-permute-done.5, bf16[1,64,32,256]{3,1,2,0:T(8,128)(2,1)S(1)} %fusion.2, bf16[3,3,64,64]{3,2,1,0:T(8,128)(2,1)S(1)} %copy-done.18), kind=kOutput, calls=%fused_computation.68 | convolution fusion | flops 67633152 | bytes 3194880 | tf_op jit(solution)/shard_map/oc,bohw->bchw/dot_general | solution.py:60
  109.9 1.8 %fusion.27 = f32[32,256,64]{1,2,0:T(8,128)} fusion(bf16[1,64,32,256]{3,1,2,0:T(8,128)(2,1)S(1)} %fusion.2, bf16[1,64,1,256]{3,1,2,0:T(8,128)(2,1)S(1)} %collective-permute-done.4, bf16[3,3,64,64]{3,2,1,0:T(8,128)(2,1)S(1)} %copy-done.18), kind=kOutput, calls=%fused_computation.56 | convolution fusion | flops 67633152 | bytes 3194880 | tf_op jit(solution)/shard_map/oc,bohw->bchw/dot_general | solution.py:60
  112.5 1.4 maximum_maximum_fusion
  117.7 0.8 copy-done.10
  118.5 1.6 fusion.24
  120.1 1.6 copy.51
  121.6 3.8 %reduce-scatter.2.cloned.1.call-done = f32[3,3,16,64]{3,2,1,0:T(8,128)} async-done(((f32[3,3,64,64]{3,2,1,0:T(8,128)}), f32[3,3,16,64]{3,2,1,0:T(8,128)}) %reduce-scatter.2.cloned.1.call-update) | async-done | bytes 36880 | tf_op jit(solution)/shard_map/reduce_scatter | solution.py:73
  125.5 30.0 %psum.40 = f32[3,3,16,64]{3,2,1,0:T(8,128)} all-reduce(f32[3,3,16,64]{3,2,1,0:T(8,128)} %reduce-scatter.2.cloned.1.call-done), channel_id=1, replica_groups=mesh['dp'=4,'row'=4,'col'=2] {'row','col'}, use_global_device_ids=true, to_apply=%region_8.0 | all-reduce | flops 9216 | bytes 73728 | tf_op jit(solution)/shard_map/psum | solution.py:72
  (84 shorter events, 17.3 us)
Async XLA Ops:
  7.2 8.3 %copy-start.8 = (bf16[1,64,32,256]{3,2,1,0:T(8,128)(2,1)S(1)}, bf16[1,64,32,256]{3,2,1,0:T(8,128)(2,1)}, u32[]{:S(2)}) copy-start(bf16[1,64,32,256]{3,2,1,0:T(8,128)(2,1)} %param.4) | copy-start | bytes 3145732
  7.2 8.3 %copy-start.18 = (bf16[3,3,64,64]{3,2,1,0:T(8,128)(2,1)S(1)}, bf16[3,3,64,64]{3,2,1,0:T(8,128)(2,1)}, u32[]{:S(2)}) copy-start(bf16[3,3,64,64]{3,2,1,0:T(8,128)(2,1)} %param.5) | copy-start | bytes 221188
  7.2 118.3 %reduce-scatter.2.cloned.1.call-start = ((), (), s32[]{:S(2)}) async-start(), calls=%async_computation.1 | async-start | bytes 368640 | tf_op jit(solution)/shard_map/reduce_scatter | solution.py:73
  9.1 17.8 %copy-start.6 = (bf16[1,64,32,256]{3,1,2,0:T(8,128)(2,1)}, bf16[1,64,32,256]{3,1,2,0:T(8,128)(2,1)S(1)}, u32[]{:S(2)}) copy-start(bf16[1,64,32,256]{3,1,2,0:T(8,128)(2,1)S(1)} %copy.26) | copy-start | bytes 3145732
  9.2 8.5 %collective-permute-start = (bf16[1,64,1,256]{3,1,2,0:T(8,128)(2,1)S(1)}, bf16[1,64,1,256]{3,1,2,0:T(8,128)(2,1)S(1)}, u32[]{:S(2)}, u32[]{:S(2)}) collective-permute-start(bf16[1,64,1,256]{3,1,2,0:T(8,128)(2,1)S(1)} %get-tuple-element.29), channel_id=1, source_target_pairs={{0,2},{2,4},{4,6},{1,3},{3,5},{5,7},{8,10},{10,12},{12,14},{9,11},... | collective-permute-start | bytes 98312 | tf_op jit(solution)/shard_map/ppermute | solution.py:14
  14.1 5.8 %collective-permute-start.1 = (bf16[1,64,1,256]{3,1,2,0:T(8,128)(2,1)S(1)}, bf16[1,64,1,256]{3,1,2,0:T(8,128)(2,1)S(1)}, u32[]{:S(2)}, u32[]{:S(2)}) collective-permute-start(bf16[1,64,1,256]{3,1,2,0:T(8,128)(2,1)S(1)} %get-tuple-element.30), channel_id=1, source_target_pairs={{2,0},{4,2},{6,4},{3,1},{5,3},{7,5},{10,8},{12,10},{14,12},{11,9},... | collective-permute-start | bytes 98312 | tf_op jit(solution)/shard_map/ppermute | solution.py:15
  20.6 8.1 %collective-permute-start.3 = (bf16[1,64,34,1]{1,2,3,0:T(8,128)(2,1)S(1)}, bf16[1,64,34,1]{1,2,3,0:T(8,128)(2,1)S(1)}, u32[]{:S(2)}, u32[]{:S(2)}) collective-permute-start(bf16[1,64,34,1]{1,2,3,0:T(8,128)(2,1)S(1)} %copy.32), channel_id=1, source_target_pairs={{1,0},{3,2},{5,4},{7,6},{9,8},{11,10},{13,12},{15,14},{17,16},{19,... | collective-permute-start | bytes 13064 | tf_op jit(solution)/shard_map/ppermute | solution.py:15
  22.2 11.0 %collective-permute-start.2 = (bf16[1,64,34,1]{1,2,3,0:T(8,128)(2,1)S(1)}, bf16[1,64,34,1]{1,2,3,0:T(8,128)(2,1)S(1)}, u32[]{:S(2)}, u32[]{:S(2)}) collective-permute-start(bf16[1,64,34,1]{1,2,3,0:T(8,128)(2,1)S(1)} %copy.29), channel_id=1, source_target_pairs={{0,1},{2,3},{4,5},{6,7},{8,9},{10,11},{12,13},{14,15},{16,17},{18,... | collective-permute-start | bytes 13064 | tf_op jit(solution)/shard_map/ppermute | solution.py:14
  29.1 4.2 %copy-start.1 = (bf16[1,64,34,1]{3,1,2,0:T(8,128)(2,1)}, bf16[1,64,34,1]{3,1,2,0:T(8,128)(2,1)S(1)}, u32[]{:S(2)}) copy-start(bf16[1,64,34,1]{3,1,2,0:T(8,128)(2,1)S(1)} %copy.33) | copy-start | bytes 13060
  33.6 1.2 copy-start.4
  33.6 1.8 %copy-start.16 = (f32[32,256,64]{1,2,0:T(8,128)S(1)}, f32[32,256,64]{1,2,0:T(8,128)}, u32[]{:S(2)}) copy-start(f32[32,256,64]{1,2,0:T(8,128)} %fusion.78) | copy-start | bytes 6291460
  33.6 2.4 %copy-start.17 = (f32[32,256,64]{1,2,0:T(8,128)S(1)}, f32[32,256,64]{1,2,0:T(8,128)}, u32[]{:S(2)}) copy-start(f32[32,256,64]{1,2,0:T(8,128)} %fusion.86) | copy-start | bytes 6291460
  34.2 2.6 %copy-start.14 = (f32[32,256,64]{1,2,0:T(8,128)S(1)}, f32[32,256,64]{1,2,0:T(8,128)}, u32[]{:S(2)}) copy-start(f32[32,256,64]{1,2,0:T(8,128)} %fusion.58) | copy-start | bytes 6291460
  34.2 3.2 %copy-start.15 = (f32[32,256,64]{1,2,0:T(8,128)S(1)}, f32[32,256,64]{1,2,0:T(8,128)}, u32[]{:S(2)}) copy-start(f32[32,256,64]{1,2,0:T(8,128)} %fusion.61) | copy-start | bytes 6291460
  34.8 2.7 %copy-start.2 = (bf16[1,64,34,1]{3,1,2,0:T(8,128)(2,1)S(1)}, bf16[1,64,34,1]{3,1,2,0:T(8,128)(2,1)}, u32[]{:S(2)}) copy-start(bf16[1,64,34,1]{3,1,2,0:T(8,128)(2,1)} %copy-done.1) | copy-start | bytes 13060
  34.8 3.5 %copy-start.11 = (f32[32,256,64]{1,2,0:T(8,128)S(1)}, f32[32,256,64]{1,2,0:T(8,128)}, u32[]{:S(2)}) copy-start(f32[32,256,64]{1,2,0:T(8,128)} %fusion.55) | copy-start | bytes 6291460
  42.1 40.9 %copy-start = (f32[32,256,64]{1,2,0:T(8,128)}, f32[32,256,64]{1,2,0:T(8,128)S(1)}, u32[]{:S(2)}) copy-start(f32[32,256,64]{1,2,0:T(8,128)S(1)} %get-tuple-element.34) | copy-start | bytes 6291460
  42.1 40.9 %copy-start.21 = (f32[64]{0:T(128)S(1)}, f32[64]{0:T(128)}, u32[]{:S(2)}) copy-start(f32[64]{0:T(128)} %param.6) | copy-start | bytes 772
  83.0 2.8 %copy-start.19 = (f32[64]{0:T(128)}, f32[64]{0:T(128)S(1)}, u32[]{:S(2)}) copy-start(f32[64]{0:T(128)S(1)} %get-tuple-element.31) | copy-start | bytes 772
  83.0 2.8 %copy-start.20 = (f32[64]{0:T(128)}, f32[64]{0:T(128)S(1)}, u32[]{:S(2)}) copy-start(f32[64]{0:T(128)S(1)} %get-tuple-element.32) | copy-start | bytes 772
  83.0 2.8 %copy-start.5 = (bf16[1,64,34,1]{3,1,2,0:T(8,128)(2,1)S(1)}, bf16[1,64,34,1]{3,1,2,0:T(8,128)(2,1)}, u32[]{:S(2)}) copy-start(bf16[1,64,34,1]{3,1,2,0:T(8,128)(2,1)} %copy-done.4) | copy-start | bytes 13060
  86.4 1.8 %copy-start.7 = (bf16[1,64,32,256]{3,1,2,0:T(8,128)(2,1)S(1)}, bf16[1,64,32,256]{3,1,2,0:T(8,128)(2,1)}, u32[]{:S(2)}) copy-start(bf16[1,64,32,256]{3,1,2,0:T(8,128)(2,1)} %copy-done.6) | copy-start | bytes 3145732
  88.3 1.1 copy-start.3
  90.0 1.2 copy-start.9
  95.0 6.6 %collective-permute-start.5 = (bf16[1,64,1,256]{3,1,2,0:T(8,128)(2,1)S(1)}, bf16[1,64,1,256]{3,1,2,0:T(8,128)(2,1)S(1)}, u32[]{:S(2)}, u32[]{:S(2)}) collective-permute-start(bf16[1,64,1,256]{3,1,2,0:T(8,128)(2,1)S(1)} %get-tuple-element.27), channel_id=1, source_target_pairs={{2,0},{4,2},{6,4},{3,1},{5,3},{7,5},{10,8},{12,10},{14,12},{11,9},... | collective-permute-start | bytes 98312 | tf_op jit(solution)/shard_map/ppermute | solution.py:15
  96.3 6.1 %collective-permute-start.4 = (bf16[1,64,1,256]{3,1,2,0:T(8,128)(2,1)S(1)}, bf16[1,64,1,256]{3,1,2,0:T(8,128)(2,1)S(1)}, u32[]{:S(2)}, u32[]{:S(2)}) collective-permute-start(bf16[1,64,1,256]{3,1,2,0:T(8,128)(2,1)S(1)} %get-tuple-element.28), channel_id=1, source_target_pairs={{0,2},{2,4},{4,6},{1,3},{3,5},{5,7},{8,10},{10,12},{12,14},{9,11},... | collective-permute-start | bytes 98312 | tf_op jit(solution)/shard_map/ppermute | solution.py:14
  103.2 8.5 %collective-permute-start.6 = (bf16[1,64,34,1]{1,2,3,0:T(8,128)(2,1)S(1)}, bf16[1,64,34,1]{1,2,3,0:T(8,128)(2,1)S(1)}, u32[]{:S(2)}, u32[]{:S(2)}) collective-permute-start(bf16[1,64,34,1]{1,2,3,0:T(8,128)(2,1)S(1)} %copy.37), channel_id=1, source_target_pairs={{1,0},{3,2},{5,4},{7,6},{9,8},{11,10},{13,12},{15,14},{17,16},{19,... | collective-permute-start | bytes 13064 | tf_op jit(solution)/shard_map/ppermute | solution.py:15
  104.8 7.3 %collective-permute-start.7 = (bf16[1,64,34,1]{1,2,3,0:T(8,128)(2,1)S(1)}, bf16[1,64,34,1]{1,2,3,0:T(8,128)(2,1)S(1)}, u32[]{:S(2)}, u32[]{:S(2)}) collective-permute-start(bf16[1,64,34,1]{1,2,3,0:T(8,128)(2,1)S(1)} %copy.41), channel_id=1, source_target_pairs={{0,1},{2,3},{4,5},{6,7},{8,9},{10,11},{12,13},{14,15},{16,17},{18,... | collective-permute-start | bytes 13064 | tf_op jit(solution)/shard_map/ppermute | solution.py:14
  115.5 1.6 copy-start.12
  115.5 2.2 %copy-start.13 = (f32[32,256,64]{1,2,0:T(8,128)S(1)}, f32[32,256,64]{1,2,0:T(8,128)}, u32[]{:S(2)}) copy-start(f32[32,256,64]{1,2,0:T(8,128)} %fusion.27) | copy-start | bytes 6291460
  116.0 2.5 %copy-start.10 = (f32[32,256,64]{1,2,0:T(8,128)S(1)}, f32[32,256,64]{1,2,0:T(8,128)}, u32[]{:S(2)}) copy-start(f32[32,256,64]{1,2,0:T(8,128)} %fusion.52) | copy-start | bytes 6291460
Sparse Core Ops, SparseCore 0:
  101.8 23.6 reduce-scatter.1
where the time goes:
time: 163 us; the launch traced here: 162 us
  blocking collectives  70.7 us (43%)
  matrix products  31.1 us (19%)
  starting transfers between devices  21 us (13%)
  between operations  14.6 us (9%)
  local copies, waits for them, and re-layouts  13.5 us (8%)
  waiting for transfers between devices  6.31 us (4%)
  other arithmetic  5.31 us (3%)
    psum x1, blocking collectives, per_device(): lax.psum((local_pre, local_sq, local_cot, local_cross), ('dp', 'row', 'co...  40.6 us
    psum x1, blocking collectives, per_device(): spatial = lax.psum(local_kernel, ('row', 'col'))  30 us
    ppermute x4, starting transfers between devices, with_halo(): before = lax.ppermute(last, axis, up)  15.8 us
    dot_general x9, matrix products, per_device(): jnp.einsum('oc,bchw->bohw', kernel[tap_row, tap_col], window, preferred_e...  15.4 us
    unnamed x48, local copies, waits for them, and re-layouts  10.1 us
    dot_general x9, matrix products, per_device(): jnp.einsum('oc,bohw->bchw', kernel[tap_row, tap_col], shifted, preferred_...  9.7 us
    dot_general x9, matrix products, per_device(): jnp.einsum('bohw,bchw->oc', pre_grad, window, preferred_element_type=jnp....  5.99 us
    ppermute x4, starting transfers between devices, with_halo(): after = lax.ppermute(initial, axis, down)  5.16 us
  transfers between devices with their start and end apart: 9, of which 3 were waited for; matrix products, arithmetic and copies ran while one was open for 15% of the time, Pallas kernels for 0%

commit v1 on v0

--- a/solution.py
+++ b/solution.py
@@ -69,7 +69,7 @@
             )
     factor = total ** (-0.5)
     local_kernel = jnp.stack(kernel_terms).reshape(3, 3, channels, channels) * factor
-    spatial = lax.psum(local_kernel, ("row", "col"))
+    spatial = lax.psum(lax.psum(local_kernel, "col"), "row")
     weight_grad = lax.psum_scatter(spatial, "dp", scatter_dimension=2, tiled=True)
     return (input_grad.astype(jnp.bfloat16), weight_grad, sum_norm / total, sum_cot / total)
 

time: 163 us -> 158 us (0.969)
  blocking collectives: 70.7 us -> 65.3 us
    psum x1 -> x2, blocking collectives: 30 us -> 24.7 us  [per_device(): spatial = lax.psum(lax.psum(local_kernel, 'col'), 'row')]
  transfers between devices with their start and end apart: 9 -> 9, of which waited for: 3 -> 3; matrix products, arithmetic and copies ran while one was open for 15% -> 16% of each run, Pallas kernels for 0% -> 0%
where the time goes in v1:
time: 158 us; the launch traced here: 157 us
  blocking collectives  65.3 us (41%)
  matrix products  31.1 us (20%)
  starting transfers between devices  21 us (13%)
  between operations  14.6 us (9%)
  local copies, waits for them, and re-layouts  13.5 us (9%)
  waiting for transfers between devices  6.3 us (4%)
  other arithmetic  5.31 us (3%)
    psum x1, blocking collectives, per_device(): lax.psum((local_pre, local_sq, local_cot, local_cross), ('dp', 'row', 'co...  40.6 us
    psum x2, blocking collectives, per_device(): spatial = lax.psum(lax.psum(local_kernel, 'col'), 'row')  24.7 us
    ppermute x4, starting transfers between devices, with_halo(): before = lax.ppermute(last, axis, up)  15.8 us
    dot_general x9, matrix products, per_device(): jnp.einsum('oc,bchw->bohw', kernel[tap_row, tap_col], window, preferred_e...  15.4 us
    unnamed x48, local copies, waits for them, and re-layouts  10.1 us
    dot_general x9, matrix products, per_device(): jnp.einsum('oc,bohw->bchw', kernel[tap_row, tap_col], shifted, preferred_...  9.75 us
    dot_general x9, matrix products, per_device(): jnp.einsum('bohw,bchw->oc', pre_grad, window, preferred_element_type=jnp....  5.99 us
    ppermute x4, starting transfers between devices, with_halo(): after = lax.ppermute(initial, axis, down)  5.16 us
  transfers between devices with their start and end apart: 9, of which 3 were waited for; matrix products, arithmetic and copies ran while one was open for 16% of the time, Pallas kernels for 0%

profile of v1, /device:TPU:0, one launch (start us, length us, event | category | flops | bytes accessed | tf_op | source)
XLA Modules:
  0.0 157.1 jit_solution(1796639763252374554)
XLA Ops:
  7.2 1.9 %copy.26 = bf16[1,64,32,256]{3,1,2,0:T(8,128)(2,1)S(1)} copy(bf16[1,64,32,256]{3,2,1,0:T(8,128)(2,1)} %param.4) | data formatting | bytes 2097152 | tf_op args[0]
  9.2 5.0 %collective-permute-start = (bf16[1,64,1,256]{3,1,2,0:T(8,128)(2,1)S(1)}, bf16[1,64,1,256]{3,1,2,0:T(8,128)(2,1)S(1)}, u32[]{:S(2)}, u32[]{:S(2)}) collective-permute-start(bf16[1,64,1,256]{3,1,2,0:T(8,128)(2,1)S(1)} %get-tuple-element.29), channel_id=1, source_target_pairs={{0,2},{2,4},{4,6},{1,3},{3,5},{5,7},{8,10},{10,12},{12,14},{9,11},... | collective-permute-start | bytes 98312 | tf_op jit(solution)/shard_map/ppermute | solution.py:14
  14.1 1.3 collective-permute-start.1
  15.4 2.2 %fusion.55 = f32[32,256,64]{1,2,0:T(8,128)} fusion(bf16[64,32,256]{2,1,0:T(8,128)(2,1)S(1)} %bitcast.222, bf16[3,3,64,64]{3,2,1,0:T(8,128)(2,1)S(1)} %copy-done.18), kind=kOutput, calls=%fused_computation.92 | convolution fusion | flops 67108864 | bytes 3162112 | tf_op jit(solution)/shard_map/oc,bchw->bohw/dot_general | solution.py:30
  18.3 1.7 %collective-permute-done.1 = bf16[1,64,1,256]{3,1,2,0:T(8,128)(2,1)S(1)} collective-permute-done((bf16[1,64,1,256]{3,1,2,0:T(8,128)(2,1)S(1)}, bf16[1,64,1,256]{3,1,2,0:T(8,128)(2,1)S(1)}, u32[]{:S(2)}, u32[]{:S(2)}) %collective-permute-start.1) | collective-permute-done | bytes 32800 | tf_op jit(solution)/shard_map/ppermute | solution.py:15
  20.6 1.3 collective-permute-start.3
  22.2 3.0 %collective-permute-start.2 = (bf16[1,64,34,1]{1,2,3,0:T(8,128)(2,1)S(1)}, bf16[1,64,34,1]{1,2,3,0:T(8,128)(2,1)S(1)}, u32[]{:S(2)}, u32[]{:S(2)}) collective-permute-start(bf16[1,64,34,1]{1,2,3,0:T(8,128)(2,1)S(1)} %copy.29), channel_id=1, source_target_pairs={{0,1},{2,3},{4,5},{6,7},{8,9},{10,11},{12,13},{14,15},{16,17},{18,... | collective-permute-start | bytes 13064 | tf_op jit(solution)/shard_map/ppermute | solution.py:14
  25.2 1.8 %fusion.58 = f32[32,256,64]{1,2,0:T(8,128)} fusion(bf16[1,64,32,256]{3,1,2,0:T(8,128)(2,1)S(1)} %copy.26, bf16[1,64,1,256]{3,1,2,0:T(8,128)(2,1)S(1)} %collective-permute-done, bf16[3,3,64,64]{3,2,1,0:T(8,128)(2,1)S(1)} %copy-done.18), kind=kOutput, calls=%fused_computation.94 | convolution fusion | flops 69206016 | bytes 3194880 | tf_op jit(solution)/shard_map/oc,bchw->bohw/dot_general | solution.py:30
  27.0 1.7 %fusion.61 = f32[32,256,64]{1,2,0:T(8,128)} fusion(bf16[1,64,1,256]{3,1,2,0:T(8,128)(2,1)S(1)} %collective-permute-done.1, bf16[1,64,32,256]{3,1,2,0:T(8,128)(2,1)S(1)} %copy.26, bf16[3,3,64,64]{3,2,1,0:T(8,128)(2,1)S(1)} %copy-done.18), kind=kOutput, calls=%fused_computation.95 | convolution fusion | flops 69206016 | bytes 3194880 | tf_op jit(solution)/shard_map/oc,bchw->bohw/dot_general | solution.py:30
  29.1 2.0 %fusion.78 = f32[32,256,64]{1,2,0:T(8,128)} fusion(bf16[3,3,64,64]{3,2,1,0:T(8,128)(2,1)S(1)} %copy-done.18, bf16[1,64,34,256]{3,1,2,0:T(8,128)(2,1)S(1)} %constant_dynamic-update-slice_fusion, bf16[1,64,34,1]{3,1,2,0:T(8,128)(2,1)S(1)} %copy.33), kind=kOutput, calls=%fused_computation.109 | convolution fusion | flops 69206016 | bytes 3784704 | tf_op jit(solution)/shard_map/oc,bchw->bohw/dot_general | solution.py:30
  31.1 2.1 %fusion.86 = f32[32,256,64]{1,2,0:T(8,128)} fusion(bf16[3,3,64,64]{3,2,1,0:T(8,128)(2,1)S(1)} %copy-done.18, bf16[1,64,34,256]{3,1,2,0:T(8,128)(2,1)S(1)} %constant_dynamic-update-slice_fusion, bf16[1,64,34,1]{3,1,2,0:T(8,128)(2,1)S(1)} %copy.33), kind=kOutput, calls=%fused_computation.117 | convolution fusion | flops 69206016 | bytes 3784704 | tf_op jit(solution)/shard_map/oc,bchw->bohw/dot_general | solution.py:30
  36.0 0.7 copy-done.14
  38.3 3.8 %fusion.3 = (f32[64]{0:T(128)S(1)}, f32[64]{0:T(128)S(1)}, f32[64]{0:T(128)S(1)}, f32[32,256,64]{1,2,0:T(8,128)S(1)}) fusion(bf16[1,64,32,256]{3,2,1,0:T(8,128)(2,1)} %param.7, bf16[1,64,34,1]{3,1,2,0:T(8,128)(2,1)S(1)} %copy-done.2, bf16[1,64,34,256]{3,1,2,0:T(8,128)(2,1)S(1)} %constant_dynamic-update-slice_fusion, ...), kind=kOutput, calls=%fused_computation.6 | convolution fusion | flops 76545856 | bytes 21611264 | tf_op jit(solution)/shard_map/oc,bchw->bohw/dot_general | solution.py:30
  42.4 40.6 %all-reduce = (f32[64]{0:T(128)S(1)}, f32[64]{0:T(128)S(1)}, f32[64]{0:T(128)S(1)}, f32[64]{0:T(128)S(1)}) all-reduce(f32[64]{0:T(128)S(1)} %get-tuple-element.13, f32[64]{0:T(128)S(1)} %reduce_sum.37, f32[64]{0:T(128)S(1)} %get-tuple-element.12, f32[64]{0:T(128)S(1)} %get-tuple-element.14), channel_id=1, replica_groups=mesh['dp'=4,'row'=4,'col'=2] {'dp','row','col'}, use_global_device_ids=true, to_apply=%region_1.0 | all-reduce | flops 256 | bytes 2048 | tf_op jit(solution)/shard_map/psum | solution.py:41
  83.1 2.8 %fusion.2 = bf16[1,64,32,256]{3,1,2,0:T(8,128)(2,1)S(1)} fusion(f32[32,256,64]{1,2,0:T(8,128)} %copy-done, f32[64]{0:T(128)S(1)} %get-tuple-element.32, f32[64]{0:T(128)S(1)} %get-tuple-element.20, f32[64]{0:T(128)S(1)} %get-tuple-element.33, f32[64]{0:T(128)S(1)} %get-tuple-element.31, f32[64]{0:T(128)S(1)} %get-tuple-element.19, ...), kind=kLoop, calls=%fused_computation.5 | loop fusion | flops 4194304 | bytes 4195584 | tf_op jit(solution)/shard_map/convert_element_type | solution.py:51
  86.5 1.8 %fusion.52 = f32[32,256,64]{1,2,0:T(8,128)} fusion(bf16[1,64,32,256]{3,1,2,0:T(8,128)(2,1)S(1)} %fusion.2, bf16[3,3,64,64]{3,2,1,0:T(8,128)(2,1)S(1)} %copy-done.18), kind=kOutput, calls=%fused_computation.89 | convolution fusion | flops 67108864 | bytes 3162112 | tf_op jit(solution)/shard_map/oc,bohw->bchw/dot_general | solution.py:60
  91.3 1.3 fusion.11
  95.0 1.3 collective-permute-start.5
  96.3 4.5 %collective-permute-start.4 = (bf16[1,64,1,256]{3,1,2,0:T(8,128)(2,1)S(1)}, bf16[1,64,1,256]{3,1,2,0:T(8,128)(2,1)S(1)}, u32[]{:S(2)}, u32[]{:S(2)}) collective-permute-start(bf16[1,64,1,256]{3,1,2,0:T(8,128)(2,1)S(1)} %get-tuple-element.28), channel_id=1, source_target_pairs={{0,2},{2,4},{4,6},{1,3},{3,5},{5,7},{8,10},{10,12},{12,14},{9,11},... | collective-permute-start | bytes 98312 | tf_op jit(solution)/shard_map/ppermute | solution.py:14
  100.9 0.8 broadcast_multiply_fusion
  101.7 0.8 collective-permute-done.4
  103.2 1.3 collective-permute-start.6
  104.8 3.2 %collective-permute-start.7 = (bf16[1,64,34,1]{1,2,3,0:T(8,128)(2,1)S(1)}, bf16[1,64,34,1]{1,2,3,0:T(8,128)(2,1)S(1)}, u32[]{:S(2)}, u32[]{:S(2)}) collective-permute-start(bf16[1,64,34,1]{1,2,3,0:T(8,128)(2,1)S(1)} %copy.41), channel_id=1, source_target_pairs={{0,1},{2,3},{4,5},{6,7},{8,9},{10,11},{12,13},{14,15},{16,17},{18,... | collective-permute-start | bytes 13064 | tf_op jit(solution)/shard_map/ppermute | solution.py:14
  108.1 1.9 %fusion.35 = f32[32,256,64]{1,2,0:T(8,128)} fusion(bf16[1,64,1,256]{3,1,2,0:T(8,128)(2,1)S(1)} %collective-permute-done.5, bf16[1,64,32,256]{3,1,2,0:T(8,128)(2,1)S(1)} %fusion.2, bf16[3,3,64,64]{3,2,1,0:T(8,128)(2,1)S(1)} %copy-done.18), kind=kOutput, calls=%fused_computation.68 | convolution fusion | flops 67633152 | bytes 3194880 | tf_op jit(solution)/shard_map/oc,bohw->bchw/dot_general | solution.py:60
  109.9 1.8 %fusion.27 = f32[32,256,64]{1,2,0:T(8,128)} fusion(bf16[1,64,32,256]{3,1,2,0:T(8,128)(2,1)S(1)} %fusion.2, bf16[1,64,1,256]{3,1,2,0:T(8,128)(2,1)S(1)} %collective-permute-done.4, bf16[3,3,64,64]{3,2,1,0:T(8,128)(2,1)S(1)} %copy-done.18), kind=kOutput, calls=%fused_computation.56 | convolution fusion | flops 67633152 | bytes 3194880 | tf_op jit(solution)/shard_map/oc,bohw->bchw/dot_general | solution.py:60
  112.5 1.4 maximum_maximum_fusion
  117.8 0.8 copy-done.10
  118.5 1.6 %fusion.24 = bf16[1,64,32,256]{3,1,2,0:T(8,128)(2,1)S(1)} fusion(f32[32,256,64]{1,2,0:T(8,128)S(1)} %copy-done.13, f32[32,256,64]{1,2,0:T(8,128)S(1)} %fusion.30, f32[32,256,64]{1,2,0:T(8,128)S(1)} %fusion.31, f32[32,256,64]{1,2,0:T(8,128)S(1)} %copy-done.10, f32[32,256,64]{1,2,0:T(8,128)S(1)} %fusion.32, f32[32,256,64]{1,2,0:T(8,128)S(1)} %fusion.33, ...), kind=kOutput, calls=%fused_computation.51 | convolution fusion | flops 71827456 | bytes 18890752 | tf_op jit(solution)/shard_map/oc,bohw->bchw/dot_general | solution.py:60
  120.1 1.6 copy.51
  121.7 3.8 %reduce-scatter.2.cloned.1.call-done = f32[3,3,16,64]{3,2,1,0:T(8,128)} async-done(((f32[3,3,64,64]{3,2,1,0:T(8,128)}), f32[3,3,16,64]{3,2,1,0:T(8,128)}) %reduce-scatter.2.cloned.1.call-update) | async-done | bytes 36880 | tf_op jit(solution)/shard_map/reduce_scatter | solution.py:73
  125.5 4.2 %psum.49 = f32[3,3,16,64]{3,2,1,0:T(8,128)S(1)} all-reduce(f32[3,3,16,64]{3,2,1,0:T(8,128)} %reduce-scatter.2.cloned.1.call-done), channel_id=1, replica_groups=mesh['dp'=4,'row'=4,'col'=2] {'col'}, use_global_device_ids=true, to_apply=%region_8.0 | all-reduce | flops 9216 | bytes 73728 | tf_op jit(solution)/shard_map/psum | solution.py:72
  129.7 20.5 %psum.48 = f32[3,3,16,64]{3,2,1,0:T(8,128)} all-reduce(f32[3,3,16,64]{3,2,1,0:T(8,128)S(1)} %psum.49), channel_id=1, replica_groups=mesh['dp'=4,'row'=4,'col'=2] {'row'}, use_global_device_ids=true, to_apply=%region_9.0 | all-reduce | flops 9216 | bytes 73728 | tf_op jit(solution)/shard_map/psum | solution.py:72
  (85 shorter events, 18.0 us)
Async XLA Ops:
  7.2 8.3 %copy-start.8 = (bf16[1,64,32,256]{3,2,1,0:T(8,128)(2,1)S(1)}, bf16[1,64,32,256]{3,2,1,0:T(8,128)(2,1)}, u32[]{:S(2)}) copy-start(bf16[1,64,32,256]{3,2,1,0:T(8,128)(2,1)} %param.4) | copy-start | bytes 3145732
  7.2 8.3 %copy-start.18 = (bf16[3,3,64,64]{3,2,1,0:T(8,128)(2,1)S(1)}, bf16[3,3,64,64]{3,2,1,0:T(8,128)(2,1)}, u32[]{:S(2)}) copy-start(bf16[3,3,64,64]{3,2,1,0:T(8,128)(2,1)} %param.5) | copy-start | bytes 221188
  7.2 118.3 %reduce-scatter.2.cloned.1.call-start = ((), (), s32[]{:S(2)}) async-start(), calls=%async_computation.1 | async-start | bytes 368640 | tf_op jit(solution)/shard_map/reduce_scatter | solution.py:73
  9.1 17.8 %copy-start.6 = (bf16[1,64,32,256]{3,1,2,0:T(8,128)(2,1)}, bf16[1,64,32,256]{3,1,2,0:T(8,128)(2,1)S(1)}, u32[]{:S(2)}) copy-start(bf16[1,64,32,256]{3,1,2,0:T(8,128)(2,1)S(1)} %copy.26) | copy-start | bytes 3145732
  9.2 8.5 %collective-permute-start = (bf16[1,64,1,256]{3,1,2,0:T(8,128)(2,1)S(1)}, bf16[1,64,1,256]{3,1,2,0:T(8,128)(2,1)S(1)}, u32[]{:S(2)}, u32[]{:S(2)}) collective-permute-start(bf16[1,64,1,256]{3,1,2,0:T(8,128)(2,1)S(1)} %get-tuple-element.29), channel_id=1, source_target_pairs={{0,2},{2,4},{4,6},{1,3},{3,5},{5,7},{8,10},{10,12},{12,14},{9,11},... | collective-permute-start | bytes 98312 | tf_op jit(solution)/shard_map/ppermute | solution.py:14
  14.1 5.8 %collective-permute-start.1 = (bf16[1,64,1,256]{3,1,2,0:T(8,128)(2,1)S(1)}, bf16[1,64,1,256]{3,1,2,0:T(8,128)(2,1)S(1)}, u32[]{:S(2)}, u32[]{:S(2)}) collective-permute-start(bf16[1,64,1,256]{3,1,2,0:T(8,128)(2,1)S(1)} %get-tuple-element.30), channel_id=1, source_target_pairs={{2,0},{4,2},{6,4},{3,1},{5,3},{7,5},{10,8},{12,10},{14,12},{11,9},... | collective-permute-start | bytes 98312 | tf_op jit(solution)/shard_map/ppermute | solution.py:15
  20.6 8.2 %collective-permute-start.3 = (bf16[1,64,34,1]{1,2,3,0:T(8,128)(2,1)S(1)}, bf16[1,64,34,1]{1,2,3,0:T(8,128)(2,1)S(1)}, u32[]{:S(2)}, u32[]{:S(2)}) collective-permute-start(bf16[1,64,34,1]{1,2,3,0:T(8,128)(2,1)S(1)} %copy.32), channel_id=1, source_target_pairs={{1,0},{3,2},{5,4},{7,6},{9,8},{11,10},{13,12},{15,14},{17,16},{19,... | collective-permute-start | bytes 13064 | tf_op jit(solution)/shard_map/ppermute | solution.py:15
  22.2 11.1 %collective-permute-start.2 = (bf16[1,64,34,1]{1,2,3,0:T(8,128)(2,1)S(1)}, bf16[1,64,34,1]{1,2,3,0:T(8,128)(2,1)S(1)}, u32[]{:S(2)}, u32[]{:S(2)}) collective-permute-start(bf16[1,64,34,1]{1,2,3,0:T(8,128)(2,1)S(1)} %copy.29), channel_id=1, source_target_pairs={{0,1},{2,3},{4,5},{6,7},{8,9},{10,11},{12,13},{14,15},{16,17},{18,... | collective-permute-start | bytes 13064 | tf_op jit(solution)/shard_map/ppermute | solution.py:14
  29.1 4.1 %copy-start.1 = (bf16[1,64,34,1]{3,1,2,0:T(8,128)(2,1)}, bf16[1,64,34,1]{3,1,2,0:T(8,128)(2,1)S(1)}, u32[]{:S(2)}) copy-start(bf16[1,64,34,1]{3,1,2,0:T(8,128)(2,1)S(1)} %copy.33) | copy-start | bytes 13060
  33.6 1.2 copy-start.4
  33.6 1.8 %copy-start.16 = (f32[32,256,64]{1,2,0:T(8,128)S(1)}, f32[32,256,64]{1,2,0:T(8,128)}, u32[]{:S(2)}) copy-start(f32[32,256,64]{1,2,0:T(8,128)} %fusion.78) | copy-start | bytes 6291460
  33.6 2.4 %copy-start.17 = (f32[32,256,64]{1,2,0:T(8,128)S(1)}, f32[32,256,64]{1,2,0:T(8,128)}, u32[]{:S(2)}) copy-start(f32[32,256,64]{1,2,0:T(8,128)} %fusion.86) | copy-start | bytes 6291460
  34.2 2.6 %copy-start.14 = (f32[32,256,64]{1,2,0:T(8,128)S(1)}, f32[32,256,64]{1,2,0:T(8,128)}, u32[]{:S(2)}) copy-start(f32[32,256,64]{1,2,0:T(8,128)} %fusion.58) | copy-start | bytes 6291460
  34.2 3.2 %copy-start.15 = (f32[32,256,64]{1,2,0:T(8,128)S(1)}, f32[32,256,64]{1,2,0:T(8,128)}, u32[]{:S(2)}) copy-start(f32[32,256,64]{1,2,0:T(8,128)} %fusion.61) | copy-start | bytes 6291460
  34.8 2.7 %copy-start.2 = (bf16[1,64,34,1]{3,1,2,0:T(8,128)(2,1)S(1)}, bf16[1,64,34,1]{3,1,2,0:T(8,128)(2,1)}, u32[]{:S(2)}) copy-start(bf16[1,64,34,1]{3,1,2,0:T(8,128)(2,1)} %copy-done.1) | copy-start | bytes 13060
  34.8 3.5 %copy-start.11 = (f32[32,256,64]{1,2,0:T(8,128)S(1)}, f32[32,256,64]{1,2,0:T(8,128)}, u32[]{:S(2)}) copy-start(f32[32,256,64]{1,2,0:T(8,128)} %fusion.55) | copy-start | bytes 6291460
  42.1 40.9 %copy-start = (f32[32,256,64]{1,2,0:T(8,128)}, f32[32,256,64]{1,2,0:T(8,128)S(1)}, u32[]{:S(2)}) copy-start(f32[32,256,64]{1,2,0:T(8,128)S(1)} %get-tuple-element.34) | copy-start | bytes 6291460
  42.1 40.9 %copy-start.21 = (f32[64]{0:T(128)S(1)}, f32[64]{0:T(128)}, u32[]{:S(2)}) copy-start(f32[64]{0:T(128)} %param.6) | copy-start | bytes 772
  83.0 2.8 %copy-start.19 = (f32[64]{0:T(128)}, f32[64]{0:T(128)S(1)}, u32[]{:S(2)}) copy-start(f32[64]{0:T(128)S(1)} %get-tuple-element.31) | copy-start | bytes 772
  83.0 2.8 %copy-start.20 = (f32[64]{0:T(128)}, f32[64]{0:T(128)S(1)}, u32[]{:S(2)}) copy-start(f32[64]{0:T(128)S(1)} %get-tuple-element.32) | copy-start | bytes 772
  83.0 2.8 %copy-start.5 = (bf16[1,64,34,1]{3,1,2,0:T(8,128)(2,1)S(1)}, bf16[1,64,34,1]{3,1,2,0:T(8,128)(2,1)}, u32[]{:S(2)}) copy-start(bf16[1,64,34,1]{3,1,2,0:T(8,128)(2,1)} %copy-done.4) | copy-start | bytes 13060
  86.4 1.9 %copy-start.7 = (bf16[1,64,32,256]{3,1,2,0:T(8,128)(2,1)S(1)}, bf16[1,64,32,256]{3,1,2,0:T(8,128)(2,1)}, u32[]{:S(2)}) copy-start(bf16[1,64,32,256]{3,1,2,0:T(8,128)(2,1)} %copy-done.6) | copy-start | bytes 3145732
  88.3 1.1 copy-start.3
  90.0 1.2 copy-start.9
  95.0 6.6 %collective-permute-start.5 = (bf16[1,64,1,256]{3,1,2,0:T(8,128)(2,1)S(1)}, bf16[1,64,1,256]{3,1,2,0:T(8,128)(2,1)S(1)}, u32[]{:S(2)}, u32[]{:S(2)}) collective-permute-start(bf16[1,64,1,256]{3,1,2,0:T(8,128)(2,1)S(1)} %get-tuple-element.27), channel_id=1, source_target_pairs={{2,0},{4,2},{6,4},{3,1},{5,3},{7,5},{10,8},{12,10},{14,12},{11,9},... | collective-permute-start | bytes 98312 | tf_op jit(solution)/shard_map/ppermute | solution.py:15
  96.3 6.1 %collective-permute-start.4 = (bf16[1,64,1,256]{3,1,2,0:T(8,128)(2,1)S(1)}, bf16[1,64,1,256]{3,1,2,0:T(8,128)(2,1)S(1)}, u32[]{:S(2)}, u32[]{:S(2)}) collective-permute-start(bf16[1,64,1,256]{3,1,2,0:T(8,128)(2,1)S(1)} %get-tuple-element.28), channel_id=1, source_target_pairs={{0,2},{2,4},{4,6},{1,3},{3,5},{5,7},{8,10},{10,12},{12,14},{9,11},... | collective-permute-start | bytes 98312 | tf_op jit(solution)/shard_map/ppermute | solution.py:14
  103.2 8.5 %collective-permute-start.6 = (bf16[1,64,34,1]{1,2,3,0:T(8,128)(2,1)S(1)}, bf16[1,64,34,1]{1,2,3,0:T(8,128)(2,1)S(1)}, u32[]{:S(2)}, u32[]{:S(2)}) collective-permute-start(bf16[1,64,34,1]{1,2,3,0:T(8,128)(2,1)S(1)} %copy.37), channel_id=1, source_target_pairs={{1,0},{3,2},{5,4},{7,6},{9,8},{11,10},{13,12},{15,14},{17,16},{19,... | collective-permute-start | bytes 13064 | tf_op jit(solution)/shard_map/ppermute | solution.py:15
  104.8 7.3 %collective-permute-start.7 = (bf16[1,64,34,1]{1,2,3,0:T(8,128)(2,1)S(1)}, bf16[1,64,34,1]{1,2,3,0:T(8,128)(2,1)S(1)}, u32[]{:S(2)}, u32[]{:S(2)}) collective-permute-start(bf16[1,64,34,1]{1,2,3,0:T(8,128)(2,1)S(1)} %copy.41), channel_id=1, source_target_pairs={{0,1},{2,3},{4,5},{6,7},{8,9},{10,11},{12,13},{14,15},{16,17},{18,... | collective-permute-start | bytes 13064 | tf_op jit(solution)/shard_map/ppermute | solution.py:14
  115.5 1.6 %copy-start.12 = (f32[32,256,64]{1,2,0:T(8,128)S(1)}, f32[32,256,64]{1,2,0:T(8,128)}, u32[]{:S(2)}) copy-start(f32[32,256,64]{1,2,0:T(8,128)} %fusion.35) | copy-start | bytes 6291460
  115.6 2.2 %copy-start.13 = (f32[32,256,64]{1,2,0:T(8,128)S(1)}, f32[32,256,64]{1,2,0:T(8,128)}, u32[]{:S(2)}) copy-start(f32[32,256,64]{1,2,0:T(8,128)} %fusion.27) | copy-start | bytes 6291460
  116.1 2.5 %copy-start.10 = (f32[32,256,64]{1,2,0:T(8,128)S(1)}, f32[32,256,64]{1,2,0:T(8,128)}, u32[]{:S(2)}) copy-start(f32[32,256,64]{1,2,0:T(8,128)} %fusion.52) | copy-start | bytes 6291460
Sparse Core Ops, SparseCore 0:
  101.8 23.6 reduce-scatter.1
